TPU v7x, 32 devices: a whole 2x2x4 slice. The times are simulated.
32 devices in a mesh: gx: 4 (over y, x), gy: 4 (over z), gz: 2 (over core).
Axes of the slice: x: 2, y: 2, z: 4, core: 2. Of those that a mesh axis runs over, the one named last changes fastest.
Arguments:
- right_side: float32 [128, 128, 256], P('gx', 'gy', 'gz'), may hold values from -1 to 1
- z_faces: float32 [256], P('gz'), may hold values from 0.5 to 2, as said below
- xy_coupling: float32 [5], replicated, as said below
- block_inverse: float32 [5, 256, 128], P(None, 'gz'), as said below
Outputs:
- solution: float32 [128, 128, 256], P('gx', 'gy', 'gz')
- residual: float32 [128, 128, 256], P('gx', 'gy', 'gz')
Inputs may be any that keep to these rules, and one draw needn't show every extreme that they name: z_faces is positive. xy_coupling[l] lies between 2.9 * 4^-l / 128^2 and 5.5 * 4^-l / 128^2. block_inverse[l] holds, block by block, the inverses of the 128 x 128 diagonal blocks of M_l built from z_faces and xy_coupling[l].
All inputs are finite; a program needn't handle non-finite values.
Results may differ from a plain program's by a relative error of at most 0.028.
Values sent between devices are 32-bit elements; how exact they have to be, the bound alone decides.
A program may use at most 128 MiB of HBM per device.

v0:
```python
import jax
import jax.numpy as jnp
from jax import lax
from jax.sharding import PartitionSpec as P

LEVELS = 5
SWEEPS = 2


damping = 0.8
highest = lax.Precision.HIGHEST


def extended(cells, sides, width):
    for axis, dim in sides:
        count = lax.axis_size(axis)
        ends = count - 1
        head = lax.slice_in_dim(cells, 0, width, axis=dim)
        tail = lax.slice_in_dim(cells, cells.shape[dim] - width, cells.shape[dim], axis=dim)
        cells = jnp.concatenate(
            [
                lax.ppermute(tail, axis, [(i, (i + 1) % count) for i in range(ends)]),
                cells,
                lax.ppermute(head, axis, [((i + 1) % count, i) for i in range(ends)]),
            ],
            axis=dim,
        )
    return cells


def interface_setup(corner_aa, corner_ab, corner_ba, corner_bb, couplings):
    determinant = corner_aa * corner_bb - corner_ab * corner_ba
    corner_inverse = (
        jnp.stack(
            [jnp.stack([corner_bb, -corner_ab], -1), jnp.stack([-corner_ba, corner_aa], -1)], -2
        )
        / determinant[:, None, None]
    )
    blocks_count = corner_aa.shape[0]
    identity = jnp.eye(blocks_count, dtype=corner_inverse.dtype)
    diagonal_part = jnp.einsum("kab,kl->kalb", corner_inverse, identity, precision=highest).reshape(
        2 * blocks_count, 2 * blocks_count
    )
    link_values = jnp.zeros((2 * blocks_count - 1,), corner_inverse.dtype).at[1::2].set(-couplings)
    schur_matrix = diagonal_part + jnp.diag(link_values, 1) + jnp.diag(link_values, -1)
    return (corner_inverse, diagonal_part, jnp.linalg.cholesky(schur_matrix))


def make_solver(inverse_block, corner_rows, couplings, device_index, down_coupling, up_coupling):
    corner_inverse, diagonal_part, factor = interface_setup(
        corner_rows[:, 0], corner_rows[:, 1], corner_rows[:, 2], corner_rows[:, 3], couplings
    )
    block_len = inverse_block.shape[0]
    forward = lax.linalg.triangular_solve(factor, diagonal_part, left_side=True, lower=True)
    reach = lax.linalg.triangular_solve(
        factor, forward, left_side=True, lower=True, transpose_a=True
    )
    padded_reach = jnp.pad(reach, ((1, 1), (0, 0)))
    slice_rows = lax.dynamic_slice_in_dim(padded_reach, 2 * device_index, 4, 0)
    needed = jnp.stack([slice_rows[0], slice_rows[3]])

    def neighbours(end_values):
        zero_carry = jnp.zeros(end_values.shape, jnp.float32)
        nearby = zero_carry + jnp.dot(
            needed, lax.all_gather(end_values, "gz", axis=0, tiled=True), precision=highest
        )
        return (nearby[0], nearby[1])

    def solve(source):
        first_extent, second_extent, depth = source.shape
        line_count = first_extent * second_extent
        local_part = jnp.einsum("xyj,ij->xyi", source, inverse_block, precision=highest)
        end_values = jnp.stack(
            [
                local_part[:, :, 0].reshape(line_count),
                local_part[:, :, block_len - 1].reshape(line_count),
            ]
        )
        below_last, above_first = neighbours(end_values)
        return (
            local_part
            + (down_coupling * below_last).reshape(first_extent, second_extent, 1)
            * inverse_block[:, 0]
            + (up_coupling * above_first).reshape(first_extent, second_extent, 1)
            * inverse_block[:, block_len - 1]
        )

    return solve


def apply_operator(iterate, lateral_weight, down_faces, up_faces):
    padded = extended(iterate, (("gx", 0), ("gy", 1), ("gz", 2)), 1)
    lateral = (
        padded[:-2, 1:-1, 1:-1]
        + padded[2:, 1:-1, 1:-1]
        + padded[1:-1, :-2, 1:-1]
        + padded[1:-1, 2:, 1:-1]
    )
    return (
        lateral_weight * (4.0 * iterate - lateral)
        + down_faces * (iterate - padded[1:-1, 1:-1, :-2])
        + up_faces * (iterate - padded[1:-1, 1:-1, 2:])
    )


def restrict(field):
    first_extent, second_extent, depth = field.shape
    return field.reshape(first_extent // 2, 2, second_extent // 2, 2, depth).sum(axis=(1, 3)) * 0.25


def prolong(padded):
    first_extent = padded.shape[0] - 2
    second_extent = padded.shape[1] - 2
    depth = padded.shape[2]
    even_rows = 0.75 * padded[1:-1] + 0.25 * padded[:-2]
    odd_rows = 0.75 * padded[1:-1] + 0.25 * padded[2:]
    widened = jnp.stack([even_rows, odd_rows], 1).reshape(
        2 * first_extent, second_extent + 2, depth
    )
    even_rows = 0.75 * widened[:, 1:-1] + 0.25 * widened[:, :-2]
    odd_rows = 0.75 * widened[:, 1:-1] + 0.25 * widened[:, 2:]
    return jnp.stack([even_rows, odd_rows], 2).reshape(2 * first_extent, 2 * second_extent, depth)


def body(right_side, z_faces, xy_coupling, block_inverse):
    device_index = lax.axis_index("gz")
    levels_count = block_inverse.shape[0]
    last_cell = block_inverse.shape[1] - 1
    corner = jnp.stack(
        [
            block_inverse[:, 0, 0],
            block_inverse[:, 0, last_cell],
            block_inverse[:, last_cell, 0],
            block_inverse[:, last_cell, last_cell],
        ],
        -1,
    )[None]
    corners, firsts = (
        lax.all_gather(corner, "gz", axis=0, tiled=True),
        lax.all_gather(z_faces[:1], "gz", axis=0, tiled=True),
    )
    couplings = firsts[1:]
    edge_faces = jnp.concatenate([firsts, jnp.ones((1,), jnp.float32)])
    top_face = lax.dynamic_slice_in_dim(edge_faces, device_index + 1, 1, 0)
    up_faces = jnp.concatenate([z_faces[1:], top_face])
    solvers = [
        make_solver(
            block_inverse[level],
            corners[:, level],
            couplings,
            device_index,
            z_faces[0],
            top_face[0],
        )
        for level in range(levels_count)
    ]

    def operator(iterate, level):
        return apply_operator(iterate, xy_coupling[level], z_faces, up_faces)

    def multigrid_cycle(source, level):
        iterate = damping * solvers[level](source)
        iterate = iterate + damping * solvers[level](source - operator(iterate, level))
        if level == LEVELS - 1:
            return iterate
        coarse = multigrid_cycle(restrict(source - operator(iterate, level)), level + 1)
        widened = extended(coarse, (("gx", 0), ("gy", 1)), 1)
        iterate = iterate + prolong(widened)
        for sweep in range(SWEEPS):
            iterate = iterate + damping * solvers[level](source - operator(iterate, level))
        return iterate

    solution = multigrid_cycle(right_side, 0)
    return (solution, right_side - operator(solution, 0))


def solution(mesh):
    return jax.shard_map(
        body,
        mesh=mesh,
        in_specs=(P("gx", "gy", "gz"), P("gz"), P(), P(None, "gz", None)),
        out_specs=(P("gx", "gy", "gz"), P("gx", "gy", "gz")),
        check_vma=False,
    )
```

profile of v0, /device:TPU:0, one launch (start us, length us, event | category | flops | bytes accessed | tf_op | source)
XLA Modules:
  0.0 584.9 jit_solution(14519528730646227863)
XLA Ops:
  27.9 4.7 collective-permute-start
  69.7 4.5 collective-permute-start.6
  75.7 4.6 collective-permute-done.7
  85.2 4.2 collective-permute-done.9
  103.8 4.8 collective-permute-start.12
  110.0 4.2 collective-permute-done.13
  137.5 4.2 collective-permute-done.19
  370.3 4.2 collective-permute-done.75
  377.7 4.2 collective-permute-done.77
  395.4 4.2 collective-permute-done.81
  402.8 4.2 collective-permute-done.83
  427.9 4.2 collective-permute-done.89
  436.6 4.2 collective-permute-done.91
  444.1 4.2 collective-permute-done.93
  462.3 4.2 collective-permute-done.97
  469.8 4.2 collective-permute-done.99
  488.0 4.2 collective-permute-done.103
  495.5 4.2 collective-permute-done.105
  505.0 4.2 collective-permute-done.107
  512.6 4.2 collective-permute-done.109
  535.1 4.2 collective-permute-done.113
  542.7 4.2 collective-permute-done.115
  565.2 4.2 collective-permute-done.119
  572.8 4.2 collective-permute-done.121
  (782 shorter events, 478.1 us)
Async XLA Ops:
  27.9 15.2 %collective-permute-start = (f32[1,32,128]{2,1,0:T(8,128)S(1)}, f32[1,32,128]{2,1,0:T(8,128)S(1)}, u32[]{:S(2)}, u32[]{:S(2)}) collective-permute-start(f32[1,32,128]{2,1,0:T(8,128)S(1)} %get-tuple-element.170), channel_id=1, source_target_pairs={{0,8},{8,16},{16,24},{1,9},{9,17},{17,25},{2,10},{10,18},{18,26},{... | collective-permute-start | bytes 49160 | tf_op jit(solution)/shard_map/ppermute | solution.py:22
  32.6 10.5 %collective-permute-start.1 = (f32[1,32,128]{2,1,0:T(8,128)S(1)}, f32[1,32,128]{2,1,0:T(8,128)S(1)}, u32[]{:S(2)}, u32[]{:S(2)}) collective-permute-start(f32[1,32,128]{2,1,0:T(8,128)S(1)} %get-tuple-element.171), channel_id=1, source_target_pairs={{8,0},{16,8},{24,16},{9,1},{17,9},{25,17},{10,2},{18,10},{26,18},{... | collective-permute-start | bytes 49160 | tf_op jit(solution)/shard_map/ppermute | solution.py:24
  46.6 5.6 collective-permute-start.3
  53.8 5.9 %collective-permute-start.5 = (f32[34,34,1]{1,2,0:T(1,128)S(1)}, f32[34,34,1]{1,2,0:T(1,128)S(1)}, u32[]{:S(2)}, u32[]{:S(2)}) collective-permute-start(f32[34,34,1]{1,2,0:T(1,128)S(1)} %copy.75), channel_id=1, source_target_pairs={{1,0},{3,2},{5,4},{7,6},{9,8},{11,10},{13,12},{15,14},{17,16},{19,... | collective-permute-start | bytes 13880 | tf_op jit(solution)/shard_map/ppermute | solution.py:24
  69.7 6.0 %collective-permute-start.6 = (f32[1,32,128]{2,1,0:T(8,128)S(1)}, f32[1,32,128]{2,1,0:T(8,128)S(1)}, u32[]{:S(2)}, u32[]{:S(2)}) collective-permute-start(f32[1,32,128]{2,1,0:T(8,128)S(1)} %get-tuple-element.168), channel_id=1, source_target_pairs={{0,8},{8,16},{16,24},{1,9},{9,17},{17,25},{2,10},{10,18},{18,26},{... | collective-permute-start | bytes 49160 | tf_op jit(solution)/shard_map/ppermute | solution.py:22
  74.3 6.0 %collective-permute-start.7 = (f32[1,32,128]{2,1,0:T(8,128)S(1)}, f32[1,32,128]{2,1,0:T(8,128)S(1)}, u32[]{:S(2)}, u32[]{:S(2)}) collective-permute-start(f32[1,32,128]{2,1,0:T(8,128)S(1)} %get-tuple-element.169), channel_id=1, source_target_pairs={{8,0},{16,8},{24,16},{9,1},{17,9},{25,17},{10,2},{18,10},{26,18},{... | collective-permute-start | bytes 49160 | tf_op jit(solution)/shard_map/ppermute | solution.py:24
  83.8 5.6 collective-permute-start.9
  103.8 6.2 %collective-permute-start.12 = (f32[1,16,128]{2,1,0:T(8,128)S(1)}, f32[1,16,128]{2,1,0:T(8,128)S(1)}, u32[]{:S(2)}, u32[]{:S(2)}) collective-permute-start(f32[1,16,128]{2,1,0:T(8,128)S(1)} %get-tuple-element.207), channel_id=1, source_target_pairs={{0,8},{8,16},{16,24},{1,9},{9,17},{17,25},{2,10},{10,18},{18,26},{... | collective-permute-start | bytes 24584 | tf_op jit(solution)/shard_map/ppermute | solution.py:22
  108.7 5.5 collective-permute-start.13
  117.7 5.6 collective-permute-start.15
  136.1 5.5 collective-permute-start.19
  143.6 5.6 collective-permute-start.21
  435.2 5.5 collective-permute-start.91
  442.7 5.6 collective-permute-start.93
  461.0 5.5 collective-permute-start.97
  468.5 5.6 collective-permute-start.99
  486.7 5.5 collective-permute-start.103
  494.2 5.6 collective-permute-start.105
  503.5 5.6 collective-permute-start.107
  511.1 5.6 collective-permute-start.109
  533.7 5.6 collective-permute-start.113
  541.3 5.6 collective-permute-start.115
  563.8 5.6 collective-permute-start.119
  571.4 5.6 collective-permute-start.121
  (146 other events, 523.7 us)
where the time goes:
time: 589 us; the launch traced here: 585 us
  starting transfers between devices  222 us (38%)
  waiting for transfers between devices  207 us (35%)
  other arithmetic  47.3 us (8%)
  local copies, waits for them, and re-layouts  39.6 us (7%)
  blocking collectives  37.1 us (6%)
  matrix products  27.5 us (5%)
    ppermute x62, waiting for transfers between devices, extended(): lax.ppermute(head, axis, [((i + 1) % count, i) for i in range(ends)])  205 us
    ppermute x62, starting transfers between devices, extended(): lax.ppermute(tail, axis, [(i, (i + 1) % count) for i in range(ends)])  141 us
    ppermute x62, starting transfers between devices, extended(): lax.ppermute(head, axis, [((i + 1) % count, i) for i in range(ends)])  80.5 us
    all_gather x18, blocking collectives, neighbours(): lax.all_gather(end_values, 'gz', axis=0, tiled=True)  32.7 us
    mul x18, other arithmetic, solve(): down_coupling * below_last  21.9 us
    dot_general x18, matrix products, solve(): jnp.einsum('xyj,ij->xyi', source, inverse_block, precision=highest)  20.1 us
  transfers between devices with their start and end apart: 124, of which 70 were waited for; matrix products, arithmetic and copies ran while one was open for 3% of the time, Pallas kernels for 0%

commit v1 on v0

--- a/solution.py
+++ b/solution.py
@@ -1,6 +1,10 @@
+import functools
+
 import jax
 import jax.numpy as jnp
 from jax import lax
+from jax.experimental import pallas as pl
+from jax.experimental.pallas import tpu as pltpu
 from jax.sharding import PartitionSpec as P
 
 LEVELS = 5
@@ -174,11 +178,616 @@
     return (solution, right_side - operator(solution, 0))
 
 
+MESH = pl.DeviceIdType.MESH
+HALOS = (4, 6, 6)
+YPAD = 8
+
+
+def block_range(offset, own, halo, extent):
+    start = offset * own - halo
+    low = max(0, start)
+    high = min(extent, (offset + 1) * own + halo)
+    return low, high - low, low - start
+
+
+def cycle_kernel(geometry, f_ref, z_ref, e_ref, g_ref, sol_ref, res_ref, *scratch):
+    gx_n, gy_n, gz_n, nx, ny, depth, levels = geometry
+    (sinv, g_all, z_all, gather) = scratch[:4]
+    R = scratch[4 : 4 + levels]
+    U = scratch[4 + levels : 4 + 2 * levels]
+    W = scratch[4 + 2 * levels : 4 + 3 * levels]
+    V = scratch[4 + 3 * levels : 4 + 4 * levels]
+    D = scratch[4 + 4 * levels : 4 + 5 * levels]
+    (own1, own2, own3, c4u, c4d, c3u, c3d, cwu, cwd) = scratch[4 + 5 * levels : 13 + 5 * levels]
+    OWN = (None, own1, own2, own3)
+    (g_send, g_recv, h_send, h_recv, a_send, a_recv, o_send, o_recv) = scratch[13 + 5 * levels :]
+
+    ix, iy, iz = lax.axis_index("gx"), lax.axis_index("gy"), lax.axis_index("gz")
+    bx = ix * gz_n + iz
+    bx_n = gx_n * gz_n
+    f32 = jnp.float32
+
+    def owned(level):
+        return nx >> level, ny >> level
+
+    def copy(src, dst, send, recv, device):
+        return pltpu.make_async_remote_copy(
+            src_ref=src,
+            dst_ref=dst,
+            send_sem=send,
+            recv_sem=recv,
+            device_id=device,
+            device_id_type=MESH,
+        )
+
+    def setup_copies(other):
+        here = (ix, iy, lax.rem(iz + other, gz_n))
+        out = []
+        for level in range(levels):
+            out.append(
+                copy(
+                    g_ref.at[level],
+                    g_all.at[level, iz],
+                    g_send.at[other, level],
+                    g_recv.at[other, level],
+                    here,
+                )
+            )
+        out.append(
+            copy(z_ref, z_all.at[iz], g_send.at[other, levels], g_recv.at[other, levels], here)
+        )
+        return out
+
+    def start_copies():
+        out = []
+        reach = -(-HALOS[0] // nx)
+        for t in range(-reach, gz_n + reach):
+            xs, xn, xd = block_range(t, nx, HALOS[0], nx * gz_n)
+            dgx, target = t // gz_n, t % gz_n
+            for dy in (-1, 0, 1):
+                ys, yn, yd = block_range(dy, ny, YPAD, ny)
+                out.append((t, dgx, target, dy, (xs, xn, xd), (ys, yn, yd)))
+        return out
+
+    plan0 = start_copies()
+
+    def copy0(entry, source_z, device):
+        t, dgx, target, dy, (xs, xn, xd), (ys, yn, yd) = entry
+        slot = (t + gz_n) * 3 + dy + 1
+        return copy(
+            f_ref.at[pl.ds(xs, xn), pl.ds(ys, yn), :],
+            R[0].at[pl.ds(xd, xn), source_z, pl.ds(yd, yn), :],
+            h_send.at[0, slot],
+            h_recv.at[0, slot, source_z],
+            device,
+        )
+
+    def inside(x, y):
+        return (x >= 0) & (x < gx_n) & (y >= 0) & (y < gy_n)
+
+    def send0(start):
+        for entry in plan0:
+            t, dgx, target, dy = entry[:4]
+            ok = inside(ix + dgx, iy + dy)
+            if dgx == 0 and dy == 0:
+                ok = ok & (iz != target)
+
+            @pl.when(ok)
+            def _():
+                c = copy0(entry, iz, (ix + dgx, iy + dy, target))
+                c.start() if start else c.wait_send()
+
+    def recv0():
+        for entry in plan0:
+            t, dgx, target, dy = entry[:4]
+            for source_z in range(gz_n):
+                if dgx == 0 and dy == 0 and source_z == target:
+                    continue
+
+                @pl.when((iz == target) & inside(ix - dgx, iy - dy))
+                def _():
+                    copy0(entry, source_z, (ix - dgx, iy - dy, source_z)).wait_recv()
+
+    send0(True)
+    for other in range(1, gz_n):
+        for c in setup_copies(other):
+            c.start()
+
+    for entry in plan0:
+        t, dgx, target, dy, (xs, xn, xd) = entry[:5]
+        if dgx == 0 and dy == 0:
+
+            @pl.when(iz == target)
+            def _():
+                def step(i, _):
+                    R[0][xd + i, target, pl.ds(YPAD, ny), :] = f_ref[xs + i]
+                    return 0
+
+                lax.fori_loop(0, xn, step, 0)
+
+    for level in range(levels):
+        g_all[level, iz] = g_ref[level]
+    z_all[iz] = z_ref[...]
+
+    for level in range(3):
+        planes, zb, rows, lanes = R[level].shape
+        halo = HALOS[level]
+        n0, n1 = owned(level)
+        reach = -(-halo // n0)
+        for t in range(1, reach + 1):
+            low = max(0, halo - t * n0)
+            high = halo - (t - 1) * n0
+            plane = jnp.zeros((high - low, zb, rows, lanes), f32)
+
+            @pl.when(bx - t < 0)
+            def _():
+                R[level][low:high] = plane
+
+            low2, high2 = planes - high, planes - low
+
+            @pl.when(bx + t >= bx_n)
+            def _():
+                R[level][low2:high2] = plane
+
+        edge = jnp.zeros((zb, YPAD, lanes), f32)
+
+        @pl.when(iy == 0)
+        def _():
+            lax.fori_loop(0, planes, lambda i, c: zero_rows(R[level], i, 0, edge), 0)
+
+        @pl.when(iy == gy_n - 1)
+        def _():
+            lax.fori_loop(0, planes, lambda i, c: zero_rows(R[level], i, rows - YPAD, edge), 0)
+
+    def fill(ref):
+        zero = jnp.zeros(ref.shape[1:], f32)
+
+        def step(i, _):
+            ref[i] = zero
+            return 0
+
+        lax.fori_loop(0, ref.shape[0], step, 0)
+
+    for ref in (c4u, c4d, c3u, c3d, cwu, cwd):
+        fill(ref)
+    for level in range(levels):
+        zero = jnp.zeros(W[level].shape[1:], f32)
+        W[level][0] = zero
+        W[level][W[level].shape[0] - 1] = zero
+
+    for other in range(1, gz_n):
+        for c in setup_copies(other):
+            c.wait()
+
+    def assemble(level, _):
+        merged = g_all[level, 0]
+        for k in range(1, gz_n):
+            block = g_all[level, k]
+            size, cz = merged.shape[0], block.shape[0]
+            face = z_all[k][:, 0:1]
+            a, d = block[0:1, 0:1], merged[size - 1 : size, size - 1 : size]
+            last, first = merged[size - 1 : size], block[0:1]
+            scale = face / (1.0 - face * face * a * d)
+            p_row = jnp.concatenate([face * a * last, first], 1) * scale
+            q_row = jnp.concatenate([last, face * d * first], 1) * scale
+            top = jnp.concatenate([merged, jnp.zeros((size, cz), f32)], 1)
+            low = jnp.concatenate([jnp.zeros((cz, size), f32), block], 1)
+            top = top + merged[:, size - 1 : size] * p_row
+            low = low + block[:, 0:1] * q_row
+            merged = jnp.concatenate([top, low], 0)
+        sinv[level] = (damping * merged).astype(jnp.bfloat16)
+        return 0
+
+    lax.fori_loop(0, levels, assemble, 0)
+
+    def plane_mask(level, i):
+        n0 = owned(level)[0]
+        x = bx * n0 - HALOS[level] + i
+        return jnp.where((x >= 0) & (x < bx_n * n0), 1.0, 0.0).astype(f32)
+
+    def row_mask(level, rows, first, stride):
+        n1 = owned(level)[1]
+        y = lax.broadcasted_iota(jnp.int32, (rows, depth), 0) * stride + first
+        y = y + iy * n1 - YPAD
+        return jnp.where((y >= 0) & (y < gy_n * n1), 1.0, 0.0).astype(f32)
+
+    def neighbours(level, i):
+        centre = W[level][i + 1]
+        rows = centre.shape[1]
+        before = pltpu.roll(centre, 1, 1)
+        after = pltpu.roll(centre, rows - 1, 1)
+        if level > 2:
+            y = lax.broadcasted_iota(jnp.int32, centre.shape, 1)
+            before = jnp.where(y > 0, before, 0.0)
+            after = jnp.where(y < rows - 1, after, 0.0)
+        return centre, W[level][i] + W[level][i + 2] + before + after
+
+    def sweep(level, first):
+        planes, zb, rows, lanes = R[level].shape
+        e = e_ref[level]
+        chunk = planes
+        while chunk % 2 == 0 and chunk * rows > 256:
+            chunk //= 2
+
+        def solve(s, _):
+            at = s * chunk
+            source = [R[level][pl.ds(at, chunk), k] for k in range(zb)]
+            flat = [v.reshape(chunk * rows, lanes) for v in source]
+            lhs = jnp.concatenate(flat, 1).astype(jnp.bfloat16)
+            out = jnp.dot(lhs, sinv[level], preferred_element_type=f32)
+            for k in range(zb):
+                w = out[:, k * lanes : (k + 1) * lanes].reshape(chunk, rows, lanes)
+                W[level][pl.ds(at + 1, chunk), k] = w
+                U[level][pl.ds(at, chunk), k] = w if first else U[level][pl.ds(at, chunk), k] + w
+                if level > 0:
+                    dd = damping * source[k] - (4.0 * e) * w
+                    D[level][pl.ds(at, chunk), k] = (
+                        dd if first else D[level][pl.ds(at, chunk), k] + dd
+                    )
+            return 0
+
+        lax.fori_loop(0, planes // chunk, solve, 0)
+
+    def update(level):
+        planes, zb, rows, lanes = R[level].shape
+        e = e_ref[level]
+        mask_y = row_mask(level, rows, 0, 1) if level < 3 else None
+
+        def step(i, _):
+            centre, total = neighbours(level, i)
+            value = (1.0 - damping) * R[level][i] + e * total
+            if level < 3:
+                value = value * (mask_y * plane_mask(level, i))[None]
+            R[level][i] = value
+            return 0
+
+        lax.fori_loop(0, planes, step, 0, unroll=2)
+
+    def restrict_planes(level, dst, planes, x0, y0):
+        rows = dst.shape[2]
+
+        def step(j, _):
+            for k in range(gz_n):
+                total = None
+                for a in (0, 1):
+                    for b in (0, 1):
+                        part = R[level][x0 + 2 * j + a, k, pl.ds(y0 + b, rows, 2), :]
+                        total = part if total is None else total + part
+                dst[j, k] = total * 0.25
+            return 0
+
+        lax.fori_loop(0, planes, step, 0)
+
+    def prolong_planes(level, src, dst, offset, x0, y0):
+        planes, zb, rows, lanes = R[level].shape
+        half = rows // 2
+        if level < 3:
+            masks = [row_mask(level, half, b, 2) for b in (0, 1)]
+
+        def step(j, _):
+            for k in range(zb):
+                def load(dx, dy):
+                    return src[x0 + j + dx, k, pl.ds(y0 + dy, half), :]
+
+                for b, dy in ((0, -1), (1, 1)):
+                    mixed = [0.75 * load(dx, 0) + 0.25 * load(dx, dy) for dx in (-1, 0, 1)]
+                    for a, far in ((0, 0), (1, 2)):
+                        value = 0.75 * mixed[1] + 0.25 * mixed[far]
+                        if level < 3:
+                            value = value * (masks[b] * plane_mask(level, 2 * j + a))
+                        dst[offset + 2 * j + a, k, pl.ds(b, half, 2), :] = value
+            return 0
+
+        lax.fori_loop(0, planes // 2, step, 0)
+
+    def correct(level, coarse_u, coarse_d, x0, y0):
+        planes = R[level].shape[0]
+        rows = R[level].shape[2]
+        e = e_ref[level]
+        prolong_planes(level, coarse_u, W[level], 1, x0, y0)
+        prolong_planes(level, coarse_d, V[level], 0, x0, y0)
+        mask_y = row_mask(level, rows, 0, 1) if level < 3 else None
+
+        def step(i, _):
+            centre, total = neighbours(level, i)
+            side = V[level][i]
+            value = R[level][i] - side - (4.0 * e) * centre + e * total
+            if level < 3:
+                value = value * (mask_y * plane_mask(level, i))[None]
+            R[level][i] = value
+            U[level][i] = U[level][i] + centre
+            if level > 0:
+                D[level][i] = D[level][i] + side
+            return 0
+
+        lax.fori_loop(0, planes, step, 0)
+
+    def exchange(level):
+        n0, n1 = owned(level)
+        halo = HALOS[level]
+        own = OWN[level]
+        reach = -(-halo // n0)
+        window = R[level]
+
+        def local(i, _):
+            window[i + halo, :, pl.ds(YPAD, n1), :] = own[i]
+            return 0
+
+        def each(act):
+            slot = 0
+            for t in range(-reach, reach + 1):
+                xs, xn, xd = block_range(t, n0, halo, n0)
+                for dy in (-1, 0, 1):
+                    if t == 0 and dy == 0:
+                        continue
+                    ys, yn, yd = block_range(dy, n1, YPAD, n1)
+                    act(t, dy, (xs, xn, xd), (ys, yn, yd), slot)
+                    slot += 1
+
+        def build(t, dy, x, y, slot):
+            there = bx + t + bx_n
+            return copy(
+                own.at[pl.ds(x[0], x[1]), :, pl.ds(y[0], y[1]), :],
+                window.at[pl.ds(x[2], x[1]), :, pl.ds(y[2], y[1]), :],
+                h_send.at[level, slot],
+                h_recv.at[level, slot, 0],
+                (there // gz_n - gx_n, iy + dy, lax.rem(there, gz_n)),
+            )
+
+        def valid(x, y):
+            return (x >= 0) & (x < bx_n) & (y >= 0) & (y < gy_n)
+
+        def start(t, dy, x, y, slot):
+            @pl.when(valid(bx + t, iy + dy))
+            def _():
+                build(t, dy, x, y, slot).start()
+
+        def finish(t, dy, x, y, slot):
+            @pl.when(valid(bx - t, iy - dy))
+            def _():
+                build(t, dy, x, y, slot).wait_recv()
+
+        def drain(t, dy, x, y, slot):
+            @pl.when(valid(bx + t, iy + dy))
+            def _():
+                build(t, dy, x, y, slot).wait_send()
+
+        each(start)
+        lax.fori_loop(0, n0, local, 0)
+        each(finish)
+        return lambda: each(drain)
+
+    def gather_all():
+        count = bx_n * gy_n
+        me = bx * gy_n + iy
+
+        def build(other, slot_x, slot_y):
+            there = other // gy_n
+            return copy(
+                own3,
+                gather.at[slot_x, slot_y],
+                a_send.at[other],
+                a_recv.at[slot_x * gy_n + slot_y],
+                (there // gz_n, lax.rem(other, gy_n), lax.rem(there, gz_n)),
+            )
+
+        def start(s, _):
+            build(lax.rem(me + s, count), bx, iy).start()
+            return 0
+
+        def finish(s, _):
+            other = lax.rem(me + s, count)
+            build(other, other // gy_n, lax.rem(other, gy_n)).wait_recv()
+            return 0
+
+        def drain(s, _):
+            build(lax.rem(me + s, count), bx, iy).wait_send()
+            return 0
+
+        lax.fori_loop(1, count, start, 0)
+        gather[bx, iy] = own3[...]
+        lax.fori_loop(1, count, finish, 0)
+        n0, n1 = owned(3)
+
+        def place(b, _):
+            for i in range(n0):
+                for y in range(gy_n):
+                    R[3][b * n0 + i, :, pl.ds(y * n1, n1), :] = gather[b, y, i]
+            return 0
+
+        lax.fori_loop(0, bx_n, place, 0)
+        return lambda: lax.fori_loop(1, count, drain, 0)
+
+    def store_padded(level, src, dst, x0):
+        rows = src.shape[2]
+
+        def step(i, _):
+            dst[x0 + i, :, pl.ds(YPAD, rows), :] = src[i]
+            return 0
+
+        lax.fori_loop(0, src.shape[0], step, 0)
+
+    recv0()
+    drains = [lambda: send0(False)]
+    for level in range(3):
+        sweep(level, True)
+        update(level)
+        sweep(level, False)
+        update(level)
+        n0 = owned(level + 1)[0]
+        restrict_planes(level, OWN[level + 1], n0, HALOS[level], YPAD)
+        drains.append(exchange(level + 1) if level < 2 else gather_all())
+    sweep(3, True)
+    update(3)
+    sweep(3, False)
+    update(3)
+    restrict_planes(3, R[4], R[4].shape[0], 0, 0)
+    sweep(4, True)
+    update(4)
+    sweep(4, False)
+    store_padded(4, U[4], c4u, 1)
+    store_padded(4, D[4], c4d, 1)
+    correct(3, c4u, c4d, 1, YPAD)
+    sweep(3, False)
+    update(3)
+    sweep(3, False)
+    pad3 = HALOS[2] // 2 + 1
+    store_padded(3, U[3], c3u, pad3)
+    store_padded(3, D[3], c3d, pad3)
+    n0, n1 = owned(3)
+    margin = YPAD // 2
+    for y in range(gy_n):
+
+        @pl.when(iy == y)
+        def _():
+            def step(j, _):
+                for src, dst in ((c3u, cwu), (c3d, cwd)):
+                    dst[j, :, pl.ds(margin, n1 + 4 * margin), :] = src[
+                        bx * n0 + j, :, pl.ds(y * n1, n1 + 4 * margin), :
+                    ]
+                return 0
+
+            lax.fori_loop(0, cwu.shape[0], step, 0)
+
+    for level in (2, 1, 0):
+        if level == 2:
+            correct(2, cwu, cwd, 1, YPAD)
+        else:
+            x0 = HALOS[level + 1] - HALOS[level] // 2
+            correct(level, U[level + 1], D[level + 1], x0, YPAD // 2)
+        sweep(level, False)
+        update(level)
+        sweep(level, False)
+
+    def out_copies(which):
+        src, dst = ((U[0], sol_ref), (R[0], res_ref))[which]
+        out = []
+        for other in range(1, gz_n):
+            there = lax.rem(iz + other, gz_n)
+            out.append(
+                copy(
+                    src.at[pl.ds(HALOS[0], nx), there, pl.ds(YPAD, ny), :],
+                    dst.at[pl.ds(iz * nx, nx), :, :],
+                    o_send.at[which, other],
+                    o_recv.at[which, other],
+                    (ix, iy, there),
+                )
+            )
+        return out
+
+    def out_local(which):
+        src, dst = ((U[0], sol_ref), (R[0], res_ref))[which]
+
+        def step(i, _):
+            dst[iz * nx + i] = src[HALOS[0] + i, iz, pl.ds(YPAD, ny), :]
+            return 0
+
+        lax.fori_loop(0, nx, step, 0)
+
+    for c in out_copies(0):
+        c.start()
+    update(0)
+    for c in out_copies(1):
+        c.start()
+    out_local(0)
+    out_local(1)
+    for drain in drains:
+        drain()
+    for which in (0, 1):
+        for c in out_copies(which):
+            c.wait()
+
+
+def zero_rows(ref, i, at, value):
+    ref[i, :, pl.ds(at, YPAD), :] = value
+    return 0
+
+
+def fits(mesh, shape, inverse_shape):
+    gx_n, gy_n, gz_n = (mesh.shape[a] for a in ("gx", "gy", "gz"))
+    nx, ny = shape[0] // (gx_n * gz_n), shape[1] // gy_n
+    return (
+        inverse_shape[0] == LEVELS == 5
+        and SWEEPS == 2
+        and inverse_shape[2] == 128
+        and nx % 8 == 0
+        and ny % 32 == 0
+        and (shape[1] >> 4) % 8 == 0
+        and gz_n <= 2
+    )
+
+
+def fused_body(mesh, right_side, z_faces, xy_coupling, block_inverse):
+    gx_n, gy_n, gz_n = (mesh.shape[a] for a in ("gx", "gy", "gz"))
+    levels, _, depth = block_inverse.shape
+    nx, ny = right_side.shape[0] // gz_n, right_side.shape[1]
+    windows = []
+    for level in range(levels):
+        if level < 3:
+            size = ((nx >> level) + 2 * HALOS[level], (ny >> level) + 2 * YPAD)
+        else:
+            size = ((nx * gx_n * gz_n) >> level, (ny * gy_n) >> level)
+        windows.append((size[0], gz_n, size[1], depth))
+    vmem = lambda shape: pltpu.VMEM(shape, jnp.float32)
+    full3, full4 = windows[3], windows[4]
+    pad3 = HALOS[2] // 2 + 1
+    c4 = (full4[0] + 2, gz_n, full4[2] + 2 * YPAD, depth)
+    c3 = (full3[0] + 2 * pad3, gz_n, full3[2] + 2 * YPAD, depth)
+    cw = (windows[2][0] // 2 + 2, gz_n, (ny >> 3) + 20, depth)
+    reach = 2 * max(-(-HALOS[k] // (nx >> k)) for k in range(3)) + 1
+    slots = 3 * max(reach, 3 * gz_n + 1)
+    dma = pltpu.SemaphoreType.DMA
+    own = lambda k: (nx >> k, gz_n, ny >> k, depth)
+    scratch = (
+        [
+            pltpu.VMEM((levels, gz_n * depth, gz_n * depth), jnp.bfloat16),
+            vmem((levels, gz_n, depth, depth)),
+            vmem((gz_n, 1, depth)),
+            vmem((gx_n * gz_n, gy_n) + own(3)),
+        ]
+        + [vmem(w) for w in windows]
+        + [vmem(w) for w in windows]
+        + [vmem((w[0] + 2,) + w[1:]) for w in windows]
+        + [vmem(w) for w in windows]
+        + [vmem(w) for w in windows]
+        + [vmem(own(1)), vmem(own(2)), vmem(own(3))]
+        + [vmem(c4), vmem(c4), vmem(c3), vmem(c3), vmem(cw), vmem(cw)]
+        + [dma((gz_n, levels + 1))] * 2
+        + [dma((3, slots)), dma((3, slots, gz_n))]
+        + [dma((gx_n * gy_n * gz_n,))] * 2
+        + [dma((2, gz_n))] * 2
+    )
+    in_vmem = pl.BlockSpec(memory_space=pltpu.VMEM)
+    return tuple(
+        pl.pallas_call(
+            functools.partial(cycle_kernel, (gx_n, gy_n, gz_n, nx, ny, depth, levels)),
+            out_shape=[jax.ShapeDtypeStruct(right_side.shape, jnp.float32)] * 2,
+            in_specs=[
+                in_vmem,
+                in_vmem,
+                pl.BlockSpec(memory_space=pltpu.SMEM),
+                in_vmem,
+            ],
+            out_specs=[in_vmem, in_vmem],
+            scratch_shapes=scratch,
+            compiler_params=pltpu.CompilerParams(
+                has_side_effects=True, vmem_limit_bytes=60 * 1024 * 1024
+            ),
+        )(right_side, z_faces.reshape(1, -1), xy_coupling, block_inverse)
+    )
+
+
 def solution(mesh):
-    return jax.shard_map(
-        body,
-        mesh=mesh,
-        in_specs=(P("gx", "gy", "gz"), P("gz"), P(), P(None, "gz", None)),
-        out_specs=(P("gx", "gy", "gz"), P("gx", "gy", "gz")),
-        check_vma=False,
-    )
+    def call(right_side, z_faces, xy_coupling, block_inverse):
+        local = body
+        if fits(mesh, right_side.shape, block_inverse.shape):
+            local = functools.partial(fused_body, mesh)
+        return jax.shard_map(
+            local,
+            mesh=mesh,
+            in_specs=(P("gx", "gy", "gz"), P("gz"), P(), P(None, "gz", None)),
+            out_specs=(P("gx", "gy", "gz"), P("gx", "gy", "gz")),
+            check_vma=False,
+        )(right_side, z_faces, xy_coupling, block_inverse)
+
+    return call

time: 589 us -> 63.6 us (0.11)
  starting transfers between devices: 222 us -> 0 us
  waiting for transfers between devices: 207 us -> 0 us
  Pallas kernels: 0 us -> 60 us
  other arithmetic: 47.3 us -> 0 us
  blocking collectives: 37.1 us -> 0 us
  local copies, waits for them, and re-layouts: 39.6 us -> 2.72 us
  matrix products: 27.5 us -> 0 us
    ppermute x124 -> x0, starting transfers between devices: 222 us -> none  [the longest x62 141 us: extended(): lax.ppermute(tail, axis, [(i, (i + 1) % count) for i in range(ends)])]
    ppermute x124 -> x0, waiting for transfers between devices: 207 us -> none  [the longest x62 205 us: extended(): lax.ppermute(head, axis, [((i + 1) % count, i) for i in range(ends)])]
    pallas_call x0 -> x1, Pallas kernels: none -> 60 us  [fused_body(): pl.pallas_call(functools.partial(cycle_kernel, (gx_n, gy_n, gz_n, nx, ny,...]
    all_gather x19 -> x0, blocking collectives: 34.5 us -> none  [the longest x18 32.7 us: neighbours(): lax.all_gather(end_values, 'gz', axis=0, tiled=True)]
    dot_general x36 -> x0, matrix products: 23.8 us -> none  [the longest x18 20.1 us: solve(): jnp.einsum('xyj,ij->xyi', source, inverse_block, precision=highest)]
    mul x23 -> x0, other arithmetic: 22.6 us -> none  [the longest x18 21.9 us: solve(): down_coupling * below_last]
    slice x84 -> x0, local copies, waits for them, and re-layouts: 15.3 us -> none  [the longest x18 4.19 us: solve(): local_part[:, :, 0].reshape(line_count)]
    another operation x56 -> x0, other arithmetic: 11.2 us -> none  [the longest x15 5.18 us: interface_setup(): return (corner_inverse, diagonal_part, jnp.linalg.cholesky(schur_matrix))]
  transfers between devices with their start and end apart: 124 -> 0, of which waited for: 70 -> 0; matrix products, arithmetic and copies ran while one was open for 3% -> 0% of each run, Pallas kernels for 0% -> 0%
where the time goes in v1:
time: 63.6 us; the launch traced here: 63.4 us
  Pallas kernels  60 us (94%)
  local copies, waits for them, and re-layouts  2.72 us (4%)
  between operations  0.65 us (1%)
    pallas_call x1, Pallas kernels, fused_body(): pl.pallas_call(functools.partial(cycle_kernel, (gx_n, gy_n, gz_n, nx, ny,...  60 us
    unnamed x4, local copies, waits for them, and re-layouts  2.72 us

profile of v1, /device:TPU:0, one launch (start us, length us, event | category | flops | bytes accessed | tf_op | source)
XLA Modules:
  0.0 63.4 jit_solution(16293604840250098938)
XLA Ops:
  0.6 60.0 %shard_map.59 = (f32[32,32,128]{2,1,0:T(8,128)}, f32[32,32,128]{2,1,0:T(8,128)}) custom-call(f32[32,32,128]{2,1,0:T(8,128)} %f_ref.1, f32[1,128]{1,0:T(1,128)} %bitcast.1, f32[5]{0:T(128)} %e_ref.1, f32[5,128,128]{2,1,0:T(8,128)} %g_ref.1), custom_call_target="tpu_custom_call" | custom-call | tf_op jit(solution)/shard_map/pallas_call | solution.py:762
  60.7 0.0 copy-start
  60.7 1.9 %copy.8 = f32[32,32,128]{2,1,0:T(8,128)} copy(f32[32,32,128]{2,1,0:T(8,128)} %get-tuple-element.4) | data formatting | bytes 1048576
  62.6 0.0 copy-done
  62.6 0.8 %copy.9 = f32[32,32,128]{2,1,0:T(8,128)} copy(f32[32,32,128]{2,1,0:T(8,128)S(1)} %copy-done) | data formatting | bytes 1048576
Async XLA Ops:
  60.7 1.9 %copy-start = (f32[32,32,128]{2,1,0:T(8,128)S(1)}, f32[32,32,128]{2,1,0:T(8,128)}, u32[]{:S(2)}) copy-start(f32[32,32,128]{2,1,0:T(8,128)} %get-tuple-element.5) | copy-start | bytes 1572868

commit v2 on v1

--- a/solution.py
+++ b/solution.py
@@ -288,10 +288,29 @@
                 def _():
                     copy0(entry, source_z, (ix - dgx, iy - dy, source_z)).wait_recv()
 
-    send0(True)
-    for other in range(1, gz_n):
-        for c in setup_copies(other):
-            c.start()
+    reach_all = max(
+        gz_n - 1 - (-HALOS[0] // nx), *[-(-HALOS[k] // owned(k)[0]) for k in (1, 2)]
+    )
+    barrier = pltpu.get_barrier_semaphore()
+
+    def greet(other, count):
+        x, y = other // gy_n, lax.rem(other, gy_n)
+        near = (jnp.abs(x - bx) <= reach_all) & (jnp.abs(y - iy) <= 1)
+        near = (near | (x == bx) | (y == iy)) & ((x != bx) | (y != iy))
+
+        @pl.when(near)
+        def _():
+            pl.semaphore_signal(
+                barrier,
+                inc=1,
+                device_id=(x // gz_n, y, lax.rem(x, gz_n)),
+                device_id_type=MESH,
+            )
+
+        return count + jnp.where(near, 1, 0).astype(jnp.int32)
+
+    partners = lax.fori_loop(0, bx_n * gy_n, greet, jnp.int32(0))
+
 
     for entry in plan0:
         t, dgx, target, dy, (xs, xn, xd) = entry[:5]
@@ -354,6 +373,12 @@
         zero = jnp.zeros(W[level].shape[1:], f32)
         W[level][0] = zero
         W[level][W[level].shape[0] - 1] = zero
+
+    pl.semaphore_wait(barrier, partners)
+    send0(True)
+    for other in range(1, gz_n):
+        for c in setup_copies(other):
+            c.start()
 
     for other in range(1, gz_n):
         for c in setup_copies(other):
@@ -558,35 +583,42 @@
         return lambda: each(drain)
 
     def gather_all():
-        count = bx_n * gy_n
-        me = bx * gy_n + iy
-
-        def build(other, slot_x, slot_y):
-            there = other // gy_n
+        def line_y(other, slot):
             return copy(
                 own3,
-                gather.at[slot_x, slot_y],
-                a_send.at[other],
-                a_recv.at[slot_x * gy_n + slot_y],
-                (there // gz_n, lax.rem(other, gy_n), lax.rem(there, gz_n)),
+                gather.at[bx, slot],
+                a_send.at[0, other],
+                a_recv.at[0, slot],
+                (ix, other, iz),
             )
 
-        def start(s, _):
-            build(lax.rem(me + s, count), bx, iy).start()
-            return 0
-
-        def finish(s, _):
-            other = lax.rem(me + s, count)
-            build(other, other // gy_n, lax.rem(other, gy_n)).wait_recv()
-            return 0
-
-        def drain(s, _):
-            build(lax.rem(me + s, count), bx, iy).wait_send()
-            return 0
-
-        lax.fori_loop(1, count, start, 0)
+        def line_x(other, slot):
+            return copy(
+                gather.at[slot],
+                gather.at[slot],
+                a_send.at[1, other],
+                a_recv.at[1, slot],
+                (other // gz_n, iy, lax.rem(other, gz_n)),
+            )
+
+        def over(build, me, count, act):
+            for s in range(1, count):
+                act(build, lax.rem(me + s, count), me)
+
+        def start(build, other, me):
+            build(other, me).start()
+
+        def finish(build, other, me):
+            build(other, other).wait_recv()
+
+        def drain(build, other, me):
+            build(other, me).wait_send()
+
+        over(line_y, iy, gy_n, start)
         gather[bx, iy] = own3[...]
-        lax.fori_loop(1, count, finish, 0)
+        over(line_y, iy, gy_n, finish)
+        over(line_x, bx, bx_n, start)
+        over(line_x, bx, bx_n, finish)
         n0, n1 = owned(3)
 
         def place(b, _):
@@ -596,7 +628,12 @@
             return 0
 
         lax.fori_loop(0, bx_n, place, 0)
-        return lambda: lax.fori_loop(1, count, drain, 0)
+
+        def drains():
+            over(line_y, iy, gy_n, drain)
+            over(line_x, bx, bx_n, drain)
+
+        return drains
 
     def store_padded(level, src, dst, x0):
         rows = src.shape[2]
@@ -754,7 +791,7 @@
         + [vmem(c4), vmem(c4), vmem(c3), vmem(c3), vmem(cw), vmem(cw)]
         + [dma((gz_n, levels + 1))] * 2
         + [dma((3, slots)), dma((3, slots, gz_n))]
-        + [dma((gx_n * gy_n * gz_n,))] * 2
+        + [dma((2, max(gx_n * gz_n, gy_n)))] * 2
         + [dma((2, gz_n))] * 2
     )
     in_vmem = pl.BlockSpec(memory_space=pltpu.VMEM)
@@ -771,7 +808,7 @@
             out_specs=[in_vmem, in_vmem],
             scratch_shapes=scratch,
             compiler_params=pltpu.CompilerParams(
-                has_side_effects=True, vmem_limit_bytes=60 * 1024 * 1024
+                collective_id=0, has_side_effects=True, vmem_limit_bytes=60 * 1024 * 1024
             ),
         )(right_side, z_faces.reshape(1, -1), xy_coupling, block_inverse)
     )

time: 63.6 us -> 59.1 us (0.929)
  Pallas kernels: 60 us -> 55.6 us
    pallas_call x1, Pallas kernels: 60 us -> 55.6 us  [fused_body(): pl.pallas_call(functools.partial(cycle_kernel, (gx_n, gy_n, gz_n, nx, ny,...]
where the time goes in v2:
time: 59.1 us; the launch traced here: 59 us
  Pallas kernels  55.6 us (94%)
  local copies, waits for them, and re-layouts  2.72 us (5%)
  between operations  0.65 us (1%)
    pallas_call x1, Pallas kernels, fused_body(): pl.pallas_call(functools.partial(cycle_kernel, (gx_n, gy_n, gz_n, nx, ny,...  55.6 us
    unnamed x4, local copies, waits for them, and re-layouts  2.72 us

profile of v2, /device:TPU:0, one launch (start us, length us, event | category | flops | bytes accessed | tf_op | source)
XLA Modules:
  0.0 59.0 jit_solution(11465422669823250201)
XLA Ops:
  0.6 55.6 %shard_map.59 = (f32[32,32,128]{2,1,0:T(8,128)}, f32[32,32,128]{2,1,0:T(8,128)}) custom-call(f32[32,32,128]{2,1,0:T(8,128)} %f_ref.1, f32[1,128]{1,0:T(1,128)} %bitcast.1, f32[5]{0:T(128)} %e_ref.1, f32[5,128,128]{2,1,0:T(8,128)} %g_ref.1), custom_call_target="tpu_custom_call" | custom-call | tf_op jit(solution)/shard_map/pallas_call | solution.py:799
  56.2 0.0 copy-start
  56.2 1.9 %copy.8 = f32[32,32,128]{2,1,0:T(8,128)} copy(f32[32,32,128]{2,1,0:T(8,128)} %get-tuple-element.4) | data formatting | bytes 1048576
  58.2 0.0 copy-done
  58.2 0.8 %copy.9 = f32[32,32,128]{2,1,0:T(8,128)} copy(f32[32,32,128]{2,1,0:T(8,128)S(1)} %copy-done) | data formatting | bytes 1048576
Async XLA Ops:
  56.2 1.9 %copy-start = (f32[32,32,128]{2,1,0:T(8,128)S(1)}, f32[32,32,128]{2,1,0:T(8,128)}, u32[]{:S(2)}) copy-start(f32[32,32,128]{2,1,0:T(8,128)} %get-tuple-element.5) | copy-start | bytes 1572868

commit v3 on v2

--- a/solution.py
+++ b/solution.py
@@ -180,6 +180,7 @@
 
 MESH = pl.DeviceIdType.MESH
 HALOS = (4, 6, 6)
+ROWS = (4, 5, 6)
 YPAD = 8
 
 
@@ -245,7 +246,8 @@
             xs, xn, xd = block_range(t, nx, HALOS[0], nx * gz_n)
             dgx, target = t // gz_n, t % gz_n
             for dy in (-1, 0, 1):
-                ys, yn, yd = block_range(dy, ny, YPAD, ny)
+                ys, yn, yd = block_range(dy, ny, ROWS[0], ny)
+                yd += YPAD - ROWS[0]
                 out.append((t, dgx, target, dy, (xs, xn, xd), (ys, yn, yd)))
         return out
 
@@ -348,6 +350,14 @@
             def _():
                 R[level][low2:high2] = plane
 
+        spare = jnp.zeros((zb, YPAD - ROWS[level], lanes), f32)
+
+        def outer(i, _):
+            R[level][i, :, pl.ds(0, YPAD - ROWS[level])] = spare
+            R[level][i, :, pl.ds(rows - YPAD + ROWS[level], YPAD - ROWS[level])] = spare
+            return 0
+
+        lax.fori_loop(0, planes, outer, 0)
         edge = jnp.zeros((zb, YPAD, lanes), f32)
 
         @pl.when(iy == 0)
@@ -427,15 +437,19 @@
             after = jnp.where(y < rows - 1, after, 0.0)
         return centre, W[level][i] + W[level][i + 2] + before + after
 
-    def sweep(level, first):
+    def sweep(level, first, margin=0):
         planes, zb, rows, lanes = R[level].shape
         e = e_ref[level]
-        chunk = planes
-        while chunk % 2 == 0 and chunk * rows > 256:
-            chunk //= 2
+
+        def widest(count):
+            return max(c for c in range(1, count + 1) if count % c == 0 and c * rows <= 300)
+
+        while margin and widest(planes - 2 * margin) * rows < 160:
+            margin -= 1
+        chunk = widest(planes - 2 * margin)
 
         def solve(s, _):
-            at = s * chunk
+            at = margin + s * chunk
             source = [R[level][pl.ds(at, chunk), k] for k in range(zb)]
             flat = [v.reshape(chunk * rows, lanes) for v in source]
             lhs = jnp.concatenate(flat, 1).astype(jnp.bfloat16)
@@ -451,9 +465,9 @@
                     )
             return 0
 
-        lax.fori_loop(0, planes // chunk, solve, 0)
-
-    def update(level):
+        lax.fori_loop(0, (planes - 2 * margin) // chunk, solve, 0)
+
+    def update(level, margin=0):
         planes, zb, rows, lanes = R[level].shape
         e = e_ref[level]
         mask_y = row_mask(level, rows, 0, 1) if level < 3 else None
@@ -466,7 +480,7 @@
             R[level][i] = value
             return 0
 
-        lax.fori_loop(0, planes, step, 0, unroll=2)
+        lax.fori_loop(margin, planes - margin, step, 0, unroll=2)
 
     def restrict_planes(level, dst, planes, x0, y0):
         rows = dst.shape[2]
@@ -505,7 +519,7 @@
 
         lax.fori_loop(0, planes // 2, step, 0)
 
-    def correct(level, coarse_u, coarse_d, x0, y0):
+    def correct(level, coarse_u, coarse_d, x0, y0, margin=0):
         planes = R[level].shape[0]
         rows = R[level].shape[2]
         e = e_ref[level]
@@ -525,7 +539,7 @@
                 D[level][i] = D[level][i] + side
             return 0
 
-        lax.fori_loop(0, planes, step, 0)
+        lax.fori_loop(margin, planes - margin, step, 0)
 
     def exchange(level):
         n0, n1 = owned(level)
@@ -545,7 +559,8 @@
                 for dy in (-1, 0, 1):
                     if t == 0 and dy == 0:
                         continue
-                    ys, yn, yd = block_range(dy, n1, YPAD, n1)
+                    ys, yn, yd = block_range(dy, n1, ROWS[level], n1)
+                    yd += YPAD - ROWS[level]
                     act(t, dy, (xs, xn, xd), (ys, yn, yd), slot)
                     slot += 1
 
@@ -647,10 +662,11 @@
     recv0()
     drains = [lambda: send0(False)]
     for level in range(3):
+        slack = HALOS[level] - ROWS[level]
         sweep(level, True)
-        update(level)
-        sweep(level, False)
-        update(level)
+        update(level, slack + 1)
+        sweep(level, False, slack + 1)
+        update(level, slack + 2)
         n0 = owned(level + 1)[0]
         restrict_planes(level, OWN[level + 1], n0, HALOS[level], YPAD)
         drains.append(exchange(level + 1) if level < 2 else gather_all())
@@ -687,14 +703,15 @@
             lax.fori_loop(0, cwu.shape[0], step, 0)
 
     for level in (2, 1, 0):
+        slack = HALOS[level] - ROWS[level]
         if level == 2:
-            correct(2, cwu, cwd, 1, YPAD)
+            correct(2, cwu, cwd, 1, YPAD, 2)
         else:
             x0 = HALOS[level + 1] - HALOS[level] // 2
-            correct(level, U[level + 1], D[level + 1], x0, YPAD // 2)
-        sweep(level, False)
-        update(level)
-        sweep(level, False)
+            correct(level, U[level + 1], D[level + 1], x0, YPAD // 2, slack + 2)
+        sweep(level, False, slack + 2)
+        update(level, slack + 3)
+        sweep(level, False, slack + 3)
 
     def out_copies(which):
         src, dst = ((U[0], sol_ref), (R[0], res_ref))[which]
@@ -723,7 +740,7 @@
 
     for c in out_copies(0):
         c.start()
-    update(0)
+    update(0, ROWS[0])
     for c in out_copies(1):
         c.start()
     out_local(0)

time: 59.1 us -> 51.5 us (0.87)
  Pallas kernels: 55.6 us -> 48 us
    pallas_call x1, Pallas kernels: 55.6 us -> 48 us  [fused_body(): pl.pallas_call(functools.partial(cycle_kernel, (gx_n, gy_n, gz_n, nx, ny,...]
where the time goes in v3:
time: 51.5 us; the launch traced here: 51.4 us
  Pallas kernels  48 us (93%)
  local copies, waits for them, and re-layouts  2.72 us (5%)
  between operations  0.65 us (1%)
    pallas_call x1, Pallas kernels, fused_body(): pl.pallas_call(functools.partial(cycle_kernel, (gx_n, gy_n, gz_n, nx, ny,...  48 us
    unnamed x4, local copies, waits for them, and re-layouts  2.72 us

profile of v3, /device:TPU:0, one launch (start us, length us, event | category | flops | bytes accessed | tf_op | source)
XLA Modules:
  0.0 51.4 jit_solution(8312900526470063194)
XLA Ops:
  0.6 48.0 %shard_map.59 = (f32[32,32,128]{2,1,0:T(8,128)}, f32[32,32,128]{2,1,0:T(8,128)}) custom-call(f32[32,32,128]{2,1,0:T(8,128)} %f_ref.1, f32[1,128]{1,0:T(1,128)} %bitcast.1, f32[5]{0:T(128)} %e_ref.1, f32[5,128,128]{2,1,0:T(8,128)} %g_ref.1), custom_call_target="tpu_custom_call" | custom-call | tf_op jit(solution)/shard_map/pallas_call | solution.py:816
  48.6 0.0 copy-start
  48.6 1.9 %copy.8 = f32[32,32,128]{2,1,0:T(8,128)} copy(f32[32,32,128]{2,1,0:T(8,128)} %get-tuple-element.4) | data formatting | bytes 1048576
  50.6 0.0 copy-done
  50.6 0.8 %copy.9 = f32[32,32,128]{2,1,0:T(8,128)} copy(f32[32,32,128]{2,1,0:T(8,128)S(1)} %copy-done) | data formatting | bytes 1048576
Async XLA Ops:
  48.6 1.9 %copy-start = (f32[32,32,128]{2,1,0:T(8,128)S(1)}, f32[32,32,128]{2,1,0:T(8,128)}, u32[]{:S(2)}) copy-start(f32[32,32,128]{2,1,0:T(8,128)} %get-tuple-element.5) | copy-start | bytes 1572868
